TPU v7x, 32 devices: a whole 2x2x4 slice. The times are simulated.
32 devices in a mesh: zero: 16 (over z, y, core), width: 2 (over x).
Axes of the slice: x: 2, y: 2, z: 4, core: 2. Of those that a mesh axis runs over, the one named last changes fastest.
Arguments:
- slopes_in: float32 [128, 128, 4096], P(None, 'zero', 'width'), may hold values from -6 to 6
- moments_in: float32 [128, 128, 4096], P(None, 'zero', 'width'), may hold values from -6 to 6
- weights_in: float32 [128, 128, 4096], P(None, 'zero', 'width'), may hold values from -0.1875 to 0.1875
Outputs:
- new_weights: float32 [128, 128, 4096], P(None, 'zero', 'width')
- new_momentum: float32 [128, 128, 4096], P(None, 'zero', 'width')
All inputs are finite; a program needn't handle non-finite values.
Results may differ from a plain program's by a relative error of at most 0.0001.
Values sent between devices are 32-bit elements; how exact they have to be, the bound alone decides.
A program may use at most 128 MiB of HBM per device.

v0:
```python
import jax
import jax.numpy as jnp
from jax import lax
from jax.sharding import PartitionSpec as P

ITERS = 3
hold_rate = 0.8
learn_rate = 0.8
decay_rate = 0.1


def body(slopes_in, moments_in, weights_in):
    new_momentum = hold_rate * moments_in + slopes_in
    direction = hold_rate * new_momentum + slopes_in
    moved = lax.all_to_all(direction, "zero", split_axis=0, concat_axis=1, tiled=True)
    total = lax.psum(jnp.sum(moved * moved, axis=(1, 2), keepdims=True), "width")
    iterate = moved * lax.rsqrt(total + 1e-06)
    for step in range(ITERS):
        gram = lax.psum(
            jnp.einsum("mik,mjk->mij", iterate, iterate, precision=lax.Precision.HIGHEST), "width"
        )
        mixed = -4.775 * gram + 2.0315 * jnp.einsum(
            "mij,mjk->mik", gram, gram, precision=lax.Precision.HIGHEST
        )
        iterate = 3.4445 * iterate + jnp.einsum(
            "mij,mjk->mik", mixed, iterate, precision=lax.Precision.HIGHEST
        )
    back = lax.all_to_all(iterate, "zero", split_axis=1, concat_axis=0, tiled=True)
    new_weights = (1.0 - learn_rate * decay_rate) * weights_in - learn_rate * back
    return (new_weights, new_momentum)


def solution(mesh):
    in_specs = (P(None, "zero", "width"), P(None, "zero", "width"), P(None, "zero", "width"))
    out_specs = (P(None, "zero", "width"), P(None, "zero", "width"))
    return jax.shard_map(body, mesh=mesh, in_specs=in_specs, out_specs=out_specs, check_vma=False)
```

profile of v0, /device:TPU:1, one launch (start us, length us, event | category | flops | bytes accessed | tf_op | source)
XLA Modules:
  0.0 609.2 jit_solution(12829300528116619400)
XLA Ops:
  7.2 9.3 %multiply_add_fusion.3 = (f32[128,8,2048]{2,1,0:T(8,128)S(1)}, f32[128,8,2048]{2,1,0:T(8,128)}) fusion(f32[128,8,2048]{2,1,0:T(8,128)} %param.3, f32[128,8,2048]{2,1,0:T(8,128)} %param.4), kind=kLoop, calls=%fused_computation.7 | loop fusion | flops 8388608 | bytes 33554432 | tf_op jit(solution)/shard_map/add | solution.py:14
  16.5 189.7 %all_to_all.27 = f32[128,8,2048]{2,1,0:T(8,128)S(1)} all-to-all(f32[128,8,2048]{2,1,0:T(8,128)S(1)} %get-tuple-element.2), channel_id=1, replica_groups=mesh['zero'=16,'width'=2] {'zero'}, dimensions={0} | all-to-all | bytes 16777216 | tf_op jit(solution)/shard_map/all_to_all | solution.py:15
  206.2 3.4 copy-done
  209.5 0.8 fusion
  210.3 4.1 psum.28
  214.4 12.9 %fusion.2 = f32[8,128,128]{2,1,0:T(8,128)} fusion(f32[16,8,8,2048]{3,2,1,0:T(8,128)} %bitcast.38, f32[8]{0:T(128)S(1)} %rsqrt_bitcast_fusion), kind=kOutput, calls=%fused_computation.10 | convolution fusion | flops 3223322624 | bytes 8912928 | tf_op jit(solution)/shard_map/mik,mjk->mij/dot_general | solution.py:20
  227.4 29.3 %all-reduce.4.cloned.1.call-done = f32[8,128,128]{2,1,0:T(8,128)} async-done(((f32[8,128,128]{2,1,0:T(8,128)}), f32[8,128,128]{2,1,0:T(8,128)}) %all-reduce.4.cloned.1.call-update) | async-done | bytes 524304 | tf_op jit(solution)/shard_map/psum | solution.py:19
  256.7 2.1 fusion.7
  258.8 11.7 %multiply_add_fusion.2 = f32[8,128,2048]{2,1,0:T(8,128)S(1)} fusion(f32[16,8,8,2048]{3,2,1,0:T(8,128)} %bitcast.39, f32[8,128,128]{2,1,0:T(8,128)S(1)} %fusion.7, f32[8]{0:T(128)S(1)} %rsqrt_bitcast_fusion), kind=kOutput, calls=%fused_computation.6 | convolution fusion | flops 3229614080 | bytes 17301536 | tf_op jit(solution)/shard_map/mij,mjk->mik/dot_general | solution.py:25
  270.5 3.4 copy-done.1
  273.9 8.5 %fusion.8 = f32[8,128,128]{2,1,0:T(8,128)} fusion(f32[8,128,2048]{2,1,0:T(8,128)S(1)} %multiply_add_fusion.2), kind=kOutput, calls=%fused_computation.21 | convolution fusion | flops 3221225472 | bytes 8912896 | tf_op jit(solution)/shard_map/mik,mjk->mij/dot_general | solution.py:20
  282.5 28.8 %all-reduce.6.cloned.1.call-done = f32[8,128,128]{2,1,0:T(8,128)} async-done(((f32[8,128,128]{2,1,0:T(8,128)}), f32[8,128,128]{2,1,0:T(8,128)}) %all-reduce.6.cloned.1.call-update) | async-done | bytes 524304 | tf_op jit(solution)/shard_map/psum | solution.py:19
  311.2 2.1 fusion.6
  313.3 14.1 %multiply_add_fusion.1 = f32[8,128,2048]{2,1,0:T(8,128)S(1)} fusion(f32[8,128,2048]{2,1,0:T(8,128)} %copy-done.1, f32[8,128,128]{2,1,0:T(8,128)S(1)} %fusion.6), kind=kOutput, calls=%fused_computation.5 | convolution fusion | flops 3225419776 | bytes 17301504 | tf_op jit(solution)/shard_map/mij,mjk->mik/dot_general | solution.py:25
  327.4 3.4 copy-done.2
  330.8 8.5 %fusion.9 = f32[8,128,128]{2,1,0:T(8,128)} fusion(f32[8,128,2048]{2,1,0:T(8,128)S(1)} %multiply_add_fusion.1), kind=kOutput, calls=%fused_computation.22 | convolution fusion | flops 3221225472 | bytes 8912896 | tf_op jit(solution)/shard_map/mik,mjk->mij/dot_general | solution.py:20
  339.4 28.8 %all-reduce.8.cloned.1.call-done = f32[8,128,128]{2,1,0:T(8,128)} async-done(((f32[8,128,128]{2,1,0:T(8,128)}), f32[8,128,128]{2,1,0:T(8,128)}) %all-reduce.8.cloned.1.call-update) | async-done | bytes 524304 | tf_op jit(solution)/shard_map/psum | solution.py:19
  368.1 2.1 fusion.5
  370.2 15.0 %multiply_add_fusion = f32[8,128,2048]{2,1,0:T(8,128)S(1)} fusion(f32[8,128,2048]{2,1,0:T(8,128)} %copy-done.2, f32[8,128,128]{2,1,0:T(8,128)S(1)} %fusion.5), kind=kOutput, calls=%fused_computation.4 | convolution fusion | flops 3225419776 | bytes 17301504 | tf_op jit(solution)/shard_map/mij,mjk->mik/dot_general | solution.py:25
  385.2 4.9 copy.8
  390.1 188.9 %all_to_all.28 = f32[8,128,2048]{2,0,1:T(8,128)S(1)} all-to-all(f32[8,128,2048]{2,0,1:T(8,128)S(1)} %copy.8), channel_id=1, replica_groups=mesh['zero'=16,'width'=2] {'zero'}, dimensions={1} | all-to-all | bytes 16777216 | tf_op jit(solution)/shard_map/all_to_all | solution.py:28
  579.0 1.8 broadcast_multiply_fusion
  580.8 9.7 %copy.9 = f32[16,8,8,2048]{3,2,1,0:T(8,128)} copy(f32[16,8,8,2048]{3,1,2,0:T(8,128)S(1)} %bitcast.40) | data formatting | bytes 16777216 | tf_op jit(solution)/shard_map/mul | solution.py:29
  590.5 12.0 %bitcast_subtract_fusion = f32[128,8,2048]{2,1,0:T(8,128)} fusion(f32[16,8,8,2048]{3,2,1,0:T(8,128)} %copy.9, f32[128,8,2048]{2,1,0:T(8,128)} %param.5), kind=kLoop, calls=%fused_computation.1 | loop fusion | flops 4194304 | bytes 25165824 | tf_op jit(solution)/shard_map/sub | solution.py:29
  (10 shorter events, 0.2 us)
Async XLA Ops:
  7.2 249.5 %all-reduce.4.cloned.1.call-start = ((), (), s32[]{:S(2)}) async-start(), calls=%async_computation.2 | async-start | bytes 1048576 | tf_op jit(solution)/shard_map/psum | solution.py:19
  206.2 3.4 copy-start
  227.3 83.9 %all-reduce.6.cloned.1.call-start = ((), (), s32[]{:S(2)}) async-start(), calls=%async_computation.3 | async-start | bytes 1048576 | tf_op jit(solution)/shard_map/psum | solution.py:19
  270.5 3.4 copy-start.1
  282.4 85.7 %all-reduce.8.cloned.1.call-start = ((), (), s32[]{:S(2)}) async-start(), calls=%async_computation.4 | async-start | bytes 1048576 | tf_op jit(solution)/shard_map/psum | solution.py:19
  327.4 3.4 copy-start.2
Sparse Core Ops, SparseCore 0:
  227.5 29.1 all-reduce.3
  282.5 28.6 all-reduce.5
  339.5 28.6 all-reduce.7
where the time goes:
time: 618 us; the launch traced here: 609 us
  blocking collectives  383 us (62%)
  waiting for transfers between devices  86.9 us (14%)
  matrix products  76.9 us (12%)
  local copies, waits for them, and re-layouts  24.7 us (4%)
  other arithmetic  23.9 us (4%)
  between operations  14 us (2%)
    all_to_all x1, blocking collectives, body(): lax.all_to_all(direction, 'zero', split_axis=0, concat_axis=1, tiled=True)  190 us
    all_to_all x1, blocking collectives, body(): lax.all_to_all(iterate, 'zero', split_axis=1, concat_axis=0, tiled=True)  189 us
    psum x3, waiting for transfers between devices, body(): lax.psum(jnp.einsum('mik,mjk->mij', iterate, iterate, precision=lax.Preci...  86.9 us
    dot_general x3, matrix products, body(): jnp.einsum('mij,mjk->mik', mixed, iterate, precision=lax.Precision.HIGHEST)  40.8 us
    dot_general x3, matrix products, body(): jnp.einsum('mik,mjk->mij', iterate, iterate, precision=lax.Precision.HIGH...  29.9 us
  transfers between devices with their start and end apart: 3, of which 3 were waited for; matrix products, arithmetic and copies ran while one was open for 0% of the time, Pallas kernels for 0%

commit v1 on v0

--- a/solution.py
+++ b/solution.py
@@ -16,8 +16,12 @@
     total = lax.psum(jnp.sum(moved * moved, axis=(1, 2), keepdims=True), "width")
     iterate = moved * lax.rsqrt(total + 1e-06)
     for step in range(ITERS):
-        gram = lax.psum(
-            jnp.einsum("mik,mjk->mij", iterate, iterate, precision=lax.Precision.HIGHEST), "width"
+        gram = jnp.sum(
+            lax.all_gather(
+                jnp.einsum("mik,mjk->mij", iterate, iterate, precision=lax.Precision.HIGHEST),
+                "width",
+            ),
+            axis=0,
         )
         mixed = -4.775 * gram + 2.0315 * jnp.einsum(
             "mij,mjk->mik", gram, gram, precision=lax.Precision.HIGHEST

time: 618 us -> 595 us (0.963)
  waiting for transfers between devices: 86.9 us -> 64.8 us
    psum x3 -> x0, waiting for transfers between devices: 86.9 us -> none  [body(): lax.psum(jnp.einsum('mik,mjk->mij', iterate, iterate, precision=lax.Preci...]
    all_gather x0 -> x3, waiting for transfers between devices: none -> 64.8 us  [body(): lax.all_gather(jnp.einsum('mik,mjk->mij', iterate, iterate, precision=lax...]
where the time goes in v1:
time: 595 us; the launch traced here: 587 us
  blocking collectives  383 us (64%)
  matrix products  72.7 us (12%)
  waiting for transfers between devices  64.8 us (11%)
  other arithmetic  27.9 us (5%)
  local copies, waits for them, and re-layouts  24.7 us (4%)
  between operations  14 us (2%)
    all_to_all x1, blocking collectives, body(): lax.all_to_all(direction, 'zero', split_axis=0, concat_axis=1, tiled=True)  190 us
    all_to_all x1, blocking collectives, body(): lax.all_to_all(iterate, 'zero', split_axis=1, concat_axis=0, tiled=True)  189 us
    all_gather x3, waiting for transfers between devices, body(): lax.all_gather(jnp.einsum('mik,mjk->mij', iterate, iterate, precision=lax...  64.8 us
    dot_general x3, matrix products, body(): jnp.einsum('mij,mjk->mik', mixed, iterate, precision=lax.Precision.HIGHEST)  40.8 us
    dot_general x3, matrix products, body(): jnp.einsum('mik,mjk->mij', iterate, iterate, precision=lax.Precision.HIGH...  30 us
    sub x1, other arithmetic, body(): (1.0 - learn_rate * decay_rate) * weights_in - learn_rate * back  12 us
  transfers between devices with their start and end apart: 3, of which 3 were waited for; matrix products, arithmetic and copies ran while one was open for 0% of the time, Pallas kernels for 0%

profile of v1, /device:TPU:1, one launch (start us, length us, event | category | flops | bytes accessed | tf_op | source)
XLA Modules:
  0.0 587.0 jit_solution(14829581679985808944)
XLA Ops:
  7.2 9.3 %multiply_add_fusion.3 = (f32[128,8,2048]{2,1,0:T(8,128)S(1)}, f32[128,8,2048]{2,1,0:T(8,128)}) fusion(f32[128,8,2048]{2,1,0:T(8,128)} %param.3, f32[128,8,2048]{2,1,0:T(8,128)} %param.4), kind=kLoop, calls=%fused_computation.7 | loop fusion | flops 8388608 | bytes 33554432 | tf_op jit(solution)/shard_map/add | solution.py:14
  16.5 189.7 %all_to_all.27 = f32[128,8,2048]{2,1,0:T(8,128)S(1)} all-to-all(f32[128,8,2048]{2,1,0:T(8,128)S(1)} %get-tuple-element.2), channel_id=1, replica_groups=mesh['zero'=16,'width'=2] {'zero'}, dimensions={0} | all-to-all | bytes 16777216 | tf_op jit(solution)/shard_map/all_to_all | solution.py:15
  206.2 3.4 copy-done
  209.5 0.8 fusion
  210.3 4.1 psum.7
  214.4 12.9 %fusion.2 = f32[8,128,128]{2,1,0:T(8,128)} fusion(f32[16,8,8,2048]{3,2,1,0:T(8,128)} %bitcast.41, f32[8]{0:T(128)S(1)} %rsqrt_bitcast_fusion), kind=kOutput, calls=%fused_computation.10 | convolution fusion | flops 3223322624 | bytes 8912928 | tf_op jit(solution)/shard_map/mik,mjk->mij/dot_general | solution.py:21
  227.4 21.9 %all-gather.7.cloned.1.call-done = f32[16,128,128]{2,1,0:T(8,128)} async-done(((f32[8,128,128]{2,1,0:T(8,128)}), f32[16,128,128]{2,1,0:T(8,128)}) %all-gather.7.cloned.1.call-update) | async-done | bytes 1048592 | tf_op jit(solution)/shard_map/all_gather | solution.py:20
  249.3 1.3 reduce_sum.37
  251.4 11.7 %multiply_add_fusion.2 = f32[8,128,2048]{2,1,0:T(8,128)S(1)} fusion(f32[16,8,8,2048]{3,2,1,0:T(8,128)} %bitcast.42, f32[8,128,128]{2,1,0:T(8,128)S(1)} %fusion.7, f32[8]{0:T(128)S(1)} %rsqrt_bitcast_fusion), kind=kOutput, calls=%fused_computation.6 | convolution fusion | flops 3229614080 | bytes 17301536 | tf_op jit(solution)/shard_map/mij,mjk->mik/dot_general | solution.py:29
  263.0 3.4 copy-done.1
  266.4 8.5 %fusion.8 = f32[8,128,128]{2,1,0:T(8,128)} fusion(f32[8,128,2048]{2,1,0:T(8,128)S(1)} %multiply_add_fusion.2), kind=kOutput, calls=%fused_computation.21 | convolution fusion | flops 3221225472 | bytes 8912896 | tf_op jit(solution)/shard_map/mik,mjk->mij/dot_general | solution.py:21
  275.0 21.4 %all-gather.9.cloned.1.call-done = f32[16,128,128]{2,1,0:T(8,128)} async-done(((f32[8,128,128]{2,1,0:T(8,128)}), f32[16,128,128]{2,1,0:T(8,128)}) %all-gather.9.cloned.1.call-update) | async-done | bytes 1048592 | tf_op jit(solution)/shard_map/all_gather | solution.py:20
  296.4 1.3 reduce_sum.38
  298.4 14.1 %multiply_add_fusion.1 = f32[8,128,2048]{2,1,0:T(8,128)S(1)} fusion(f32[8,128,2048]{2,1,0:T(8,128)} %copy-done.1, f32[8,128,128]{2,1,0:T(8,128)S(1)} %fusion.6), kind=kOutput, calls=%fused_computation.5 | convolution fusion | flops 3225419776 | bytes 17301504 | tf_op jit(solution)/shard_map/mij,mjk->mik/dot_general | solution.py:29
  312.6 3.4 copy-done.2
  315.9 8.5 %fusion.9 = f32[8,128,128]{2,1,0:T(8,128)} fusion(f32[8,128,2048]{2,1,0:T(8,128)S(1)} %multiply_add_fusion.1), kind=kOutput, calls=%fused_computation.22 | convolution fusion | flops 3221225472 | bytes 8912896 | tf_op jit(solution)/shard_map/mik,mjk->mij/dot_general | solution.py:21
  324.5 21.4 %all-gather.11.cloned.1.call-done = f32[16,128,128]{2,1,0:T(8,128)} async-done(((f32[8,128,128]{2,1,0:T(8,128)}), f32[16,128,128]{2,1,0:T(8,128)}) %all-gather.11.cloned.1.call-update) | async-done | bytes 1048592 | tf_op jit(solution)/shard_map/all_gather | solution.py:20
  345.9 1.3 reduce_sum.39
  347.9 15.0 %multiply_add_fusion = f32[8,128,2048]{2,1,0:T(8,128)S(1)} fusion(f32[8,128,2048]{2,1,0:T(8,128)} %copy-done.2, f32[8,128,128]{2,1,0:T(8,128)S(1)} %fusion.5), kind=kOutput, calls=%fused_computation.4 | convolution fusion | flops 3225419776 | bytes 17301504 | tf_op jit(solution)/shard_map/mij,mjk->mik/dot_general | solution.py:29
  363.0 4.9 copy.8
  367.8 188.9 %all_to_all.28 = f32[8,128,2048]{2,0,1:T(8,128)S(1)} all-to-all(f32[8,128,2048]{2,0,1:T(8,128)S(1)} %copy.8), channel_id=1, replica_groups=mesh['zero'=16,'width'=2] {'zero'}, dimensions={1} | all-to-all | bytes 16777216 | tf_op jit(solution)/shard_map/all_to_all | solution.py:32
  556.7 1.8 broadcast_multiply_fusion
  558.5 9.7 %copy.9 = f32[16,8,8,2048]{3,2,1,0:T(8,128)} copy(f32[16,8,8,2048]{3,1,2,0:T(8,128)S(1)} %bitcast.43) | data formatting | bytes 16777216 | tf_op jit(solution)/shard_map/mul | solution.py:33
  568.3 12.0 %bitcast_subtract_fusion = f32[128,8,2048]{2,1,0:T(8,128)} fusion(f32[16,8,8,2048]{3,2,1,0:T(8,128)} %copy.9, f32[128,8,2048]{2,1,0:T(8,128)} %param.5), kind=kLoop, calls=%fused_computation.1 | loop fusion | flops 4194304 | bytes 25165824 | tf_op jit(solution)/shard_map/sub | solution.py:33
  (13 shorter events, 2.2 us)
Async XLA Ops:
  7.2 242.2 %all-gather.7.cloned.1.call-start = ((), (), s32[]{:S(2)}) async-start(), calls=%async_computation.2 | async-start | bytes 1572864 | tf_op jit(solution)/shard_map/all_gather | solution.py:20
  206.2 3.4 copy-start
  227.3 69.1 %all-gather.9.cloned.1.call-start = ((), (), s32[]{:S(2)}) async-start(), calls=%async_computation.3 | async-start | bytes 1572864 | tf_op jit(solution)/shard_map/all_gather | solution.py:20
  263.0 3.4 copy-start.1
  275.0 71.0 %all-gather.11.cloned.1.call-start = ((), (), s32[]{:S(2)}) async-start(), calls=%async_computation.4 | async-start | bytes 1572864 | tf_op jit(solution)/shard_map/all_gather | solution.py:20
  312.5 3.4 copy-start.2
Sparse Core Ops, SparseCore 0:
  227.5 21.8 all-gather.6
  275.1 21.2 all-gather.8
  324.6 21.2 all-gather.10
